TPU v7x, 32 devices: a whole 2x2x4 slice. The times are simulated.
32 devices in a mesh: gx: 8 (over z, x), gy: 4 (over y, core).
Axes of the slice: x: 2, y: 2, z: 4, core: 2. Of those that a mesh axis runs over, the one named last changes fastest.
Arguments:
- image: float32 [32, 128, 512], P(None, 'gx', 'gy'), may hold values from -6 to 6
Outputs:
- likelihood: float32 [32, 128, 512], P(None, 'gx', 'gy')
All inputs are finite; a program needn't handle non-finite values.
Results may differ from a plain program's by a relative error of at most 0.0003.
Values sent between devices are 32-bit elements; how exact they have to be, the bound alone decides.
A program may use at most 64 MiB of HBM per device.

v0:
```python
import functools

import jax
import jax.numpy as jnp
from jax import lax
from jax.experimental import pallas as pl
from jax.experimental.pallas import tpu as pltpu
from jax.sharding import PartitionSpec as P

DIP_HALF = 4
STRIKE_HALF = 8
EPSILON = 1e-06
LANES = 128
TILE = 8
CHUNK = 8
F32 = jnp.float32


def band_matrix():
    position = lax.broadcasted_iota(jnp.int32, (2 * LANES, LANES), 0)
    position = jnp.where(position < LANES + LANES // 2, position, position - 2 * LANES)
    distance = position - lax.broadcasted_iota(jnp.int32, (2 * LANES, LANES), 1)
    return jnp.where(jnp.abs(distance) <= STRIKE_HALF, 1.0, 0.0).astype(jnp.bfloat16)


def band_sum(values, band):
    high = values.astype(jnp.bfloat16)
    low = (values - high.astype(F32)).astype(jnp.bfloat16)
    return jnp.dot(high, band, preferred_element_type=F32) + jnp.dot(
        low, band, preferred_element_type=F32
    )


def ring_roll(main, halo, z, left, both):
    lane = lax.broadcasted_iota(jnp.int32, main.shape, 1)
    if left:
        shift = lax.rem(LANES - z, LANES)
        keep = lane < LANES - z
    else:
        shift = z
        keep = lane >= z
    main = pltpu.roll(main, shift, 1)
    halo = pltpu.roll(halo, shift, 1)
    moved = jnp.where(keep, main, halo)
    return (moved, jnp.where(keep, halo, main)) if both else moved


def row_windows(rows, count):
    total = rows.shape[0]
    width = rows
    for step in (1, 2, 4):
        width = width + pltpu.roll(width, total - step, 0)
    return (
        width[:count] + width[STRIKE_HALF : STRIKE_HALF + count]
        + rows[2 * STRIKE_HALF : 2 * STRIKE_HALF + count]
    )


def dip_window(planes):
    two = [a + b for a, b in zip(planes[:-1], planes[1:])]
    four = [a + b for a, b in zip(two[:-2], two[2:])]
    eight = [a + b for a, b in zip(four[:-4], four[4:])]
    return [a + b for a, b in zip(eight[:CHUNK], planes[8:])]


def column(ref, base, first, rows):
    return [ref[base + j, pl.ds(first, rows), :] for j in range(CHUNK + 2 * DIP_HALF)]


def prepare_own(chunk, rows, main_ref, halo_ref, box_ref, shear_refs, band):
    own = rows - 2 * STRIKE_HALF
    at = pl.ds(STRIKE_HALF, own)
    base = chunk * CHUNK
    squares = []
    for i in range(CHUNK):
        z = base + i
        main = main_ref[z + DIP_HALF, at, :]
        halo = halo_ref[z + DIP_HALF, at, :]
        squares.append(jnp.concatenate([main * main, halo * halo], axis=1))
        for left, (s_main, s_halo) in ((True, shear_refs[0]), (False, shear_refs[1])):
            s_main[z + DIP_HALF, at, :], s_halo[z + DIP_HALF, at, :] = ring_roll(
                main, halo, z, left, True
            )
    boxed = band_sum(jnp.concatenate(squares, axis=0), band)
    for i in range(CHUNK):
        box_ref[base + i + DIP_HALF, at, :] = boxed[i * own : (i + 1) * own]


def ratio(numerator, denominator):
    return numerator / ((2 * DIP_HALF + 1) * denominator + EPSILON)


def sheared_squares(s_main, s_halo, base, firsts, left):
    tiles = [
        (dip_window(column(s_main, base, t, TILE)), dip_window(column(s_halo, base, t, TILE)))
        for t in firsts
    ]
    result = []
    for i in range(CHUNK):
        amp = ring_roll(
            jnp.concatenate([tile[0][i] for tile in tiles], axis=0),
            jnp.concatenate([tile[1][i] for tile in tiles], axis=0),
            base + i, not left, False,
        )
        result.append(amp * amp)
    return result


def finish_own(chunk, rows, main_ref, halo_ref, box_ref, shear_refs, square_refs, band, out_ref):
    own = rows - 2 * STRIKE_HALF
    first = STRIKE_HALF
    base = chunk * CHUNK
    squares = [[], []]
    for ref, into in ((main_ref, squares[0]), (halo_ref, squares[1])):
        tiles = [dip_window(column(ref, base, t, TILE)) for t in range(first, first + own, TILE)]
        for i in range(CHUNK):
            amp = jnp.concatenate([tile[i] for tile in tiles], axis=0)
            into.append(amp * amp)
    for i in range(CHUNK):
        square_refs[0][base + i] = squares[0][i]
    numerators = band_sum(
        jnp.concatenate([jnp.concatenate(pair, axis=1) for pair in zip(*squares)], axis=0), band
    )
    denominators = dip_window(column(box_ref, base, first, own))
    for i in range(CHUNK):
        out_ref[base + i] = ratio(numerators[i * own : (i + 1) * own], denominators[i])
    for left, (s_main, s_halo), square in (
        (True, shear_refs[0], square_refs[1]), (False, shear_refs[1], square_refs[2])
    ):
        values = sheared_squares(s_main, s_halo, base, range(first, first + own, TILE), left)
        for i in range(CHUNK):
            square[base + i] = values[i]


def prepare(chunk, rows, main_ref, halo_ref, box_ref, row_ref, shear_refs, shear_row_refs, band):
    own = rows - 2 * STRIKE_HALF
    w = STRIKE_HALF
    base = chunk * CHUNK
    squares = []

    def edges(values):
        return jnp.concatenate([values[:w], values[w + own :]], axis=0)

    for i in range(CHUNK):
        z = base + i
        main = main_ref[z + DIP_HALF]
        halo = halo_ref[z + DIP_HALF]
        main_sq = main * main
        halo_sq = halo * halo
        squares.append(jnp.concatenate([edges(main_sq), edges(halo_sq)], axis=1))
        main_row = row_windows(main_sq, own)
        halo_row = row_windows(halo_sq, own)
        row_ref[z + DIP_HALF] = main_row
        for left, (s_main, s_halo), (r_main, r_halo) in (
            (True, shear_refs[0], shear_row_refs[0]),
            (False, shear_refs[1], shear_row_refs[1]),
        ):
            a, b = ring_roll(edges(main), edges(halo), z, left, True)
            for ref, value in ((s_main, a), (s_halo, b)):
                ref[z + DIP_HALF, pl.ds(0, w), :] = value[:w]
                ref[z + DIP_HALF, pl.ds(w + own, w), :] = value[w:]
            a, b = ring_roll(main_row, halo_row, z, left, True)
            r_main[z + DIP_HALF] = a
            r_halo[z + DIP_HALF] = b
    boxed = band_sum(jnp.concatenate(squares, axis=0), band)
    for i in range(CHUNK):
        at = i * 2 * w
        box_ref[base + i + DIP_HALF, pl.ds(0, w), :] = boxed[at : at + w]
        box_ref[base + i + DIP_HALF, pl.ds(w + own, w), :] = boxed[at + w : at + 2 * w]


def finish(
    chunk, rows, main_ref, halo_ref, box_ref, row_ref, shear_refs, shear_row_refs, square_refs,
    band, out_ref,
):
    own = rows - 2 * STRIKE_HALF
    base = chunk * CHUNK
    first = STRIKE_HALF
    best = [out_ref[base + i] for i in range(CHUNK)]

    def combine(i, numerator, denominator):
        best[i] = jnp.minimum(best[i], ratio(numerator, denominator))

    def sloped(ref, i, incline):
        total = None
        for d in range(-DIP_HALF, DIP_HALF + 1):
            term = ref[base + i + DIP_HALF + d, pl.ds(first + incline * d, own), :]
            total = term if total is None else total + term
        return total

    top = dip_window(column(main_ref, base, 0, first))
    bottom = dip_window(column(main_ref, base, first + own, first))
    denominators = dip_window(column(row_ref, base, 0, own))
    for i in range(CHUNK):
        amp_sq = jnp.concatenate(
            [top[i] * top[i], square_refs[0][base + i], bottom[i] * bottom[i]], axis=0
        )
        combine(i, row_windows(amp_sq, own), denominators[i])

    for incline in (-1, 1):
        squares = []
        for i in range(CHUNK):
            amp = sloped(main_ref, i, incline)
            halo = sloped(halo_ref, i, incline)
            squares.append(jnp.concatenate([amp * amp, halo * halo], axis=1))
        numerators = band_sum(jnp.concatenate(squares, axis=0), band)
        for i in range(CHUNK):
            combine(i, numerators[i * own : (i + 1) * own], sloped(box_ref, i, incline))

    for left, (s_main, s_halo), (r_main, r_halo), square in (
        (True, shear_refs[0], shear_row_refs[0], square_refs[1]),
        (False, shear_refs[1], shear_row_refs[1], square_refs[2]),
    ):
        values = sheared_squares(s_main, s_halo, base, (0, first + own), left)
        row_tiles = [
            (dip_window(column(r_main, base, t, TILE)), dip_window(column(r_halo, base, t, TILE)))
            for t in range(0, own, TILE)
        ]
        for i in range(CHUNK):
            denominator = ring_roll(
                jnp.concatenate([tile[0][i] for tile in row_tiles], axis=0),
                jnp.concatenate([tile[1][i] for tile in row_tiles], axis=0),
                base + i, not left, False,
            )
            amp_sq = jnp.concatenate(
                [values[i][:first], square[base + i], values[i][first:]], axis=0
            )
            combine(i, row_windows(amp_sq, own), denominator)

    for i in range(CHUNK):
        out_ref[base + i] = best[i]


SIDE = STRIKE_HALF
GROUP = LANES // SIDE
MESH = pl.DeviceIdType.MESH


def kernel(
    count_x, count_y, image_ref, out_ref, main, halo, box, row,
    sl_m, sl_h, sr_m, sr_h, rl_m, rl_h, rr_m, rr_h, square_0, square_1, square_2,
    pack_first, pack_last, after, before, send_x, recv_x, send_s, recv_s, load_sem,
):
    depth, own, _ = image_ref.shape
    rows = own + 2 * STRIKE_HALF
    chunks = depth // CHUNK
    w = STRIKE_HALF
    body = pl.ds(DIP_HALF, depth)
    mine = main.at[body, pl.ds(w, own), :]
    load = pltpu.make_async_copy(image_ref, mine, load_sem)
    load.start()
    gx = lax.axis_index("gx")
    gy = lax.axis_index("gy")
    exists = {
        (dx, dy): jnp.logical_and(
            jnp.logical_and(gx + dx >= 0, gx + dx < count_x),
            jnp.logical_and(gy + dy >= 0, gy + dy < count_y),
        )
        for dx in (-1, 0, 1) for dy in (-1, 0, 1) if (dx, dy) != (0, 0)
    }

    def device(dx, dy):
        return (lax.rem(gx + dx + count_x, count_x), lax.rem(gy + dy + count_y, count_y))

    edge = jnp.zeros((depth, w, LANES), F32)
    main[body, pl.ds(0, w), :] = edge
    main[body, pl.ds(w + own, w), :] = edge
    after[...] = jnp.zeros(after.shape, F32)
    before[...] = jnp.zeros(before.shape, F32)
    barrier = pltpu.get_barrier_semaphore()
    faces = {key: there for key, there in exists.items() if 0 in key}
    for (dx, dy), there in faces.items():
        @pl.when(there)
        def _(dx=dx, dy=dy):
            pl.semaphore_signal(barrier, inc=1, device_id=device(dx, dy), device_id_type=MESH)

    for ref in (main, halo, box, row, sl_m, sl_h, sr_m, sr_h, rl_m, rl_h, rr_m, rr_h):
        zeros = jnp.zeros((DIP_HALF,) + ref.shape[1:], F32)
        ref[pl.ds(0, DIP_HALF)] = zeros
        ref[pl.ds(depth + DIP_HALF, DIP_HALF)] = zeros
    load.wait()

    lane = lax.broadcasted_iota(jnp.int32, (own, LANES), 1)
    for q in range(depth // GROUP):
        first = main[q * GROUP + DIP_HALF, pl.ds(w, own), :]
        last = pltpu.roll(main[q * GROUP + DIP_HALF, pl.ds(w, own), :], SIDE, 1)
        for j in range(1, GROUP):
            plane = main[q * GROUP + j + DIP_HALF, pl.ds(w, own), :]
            first = jnp.where(lane >= SIDE * j, pltpu.roll(plane, SIDE * j, 1), first)
            last = jnp.where(
                lane >= SIDE * j, pltpu.roll(plane, (SIDE * j + SIDE) % LANES, 1), last
            )
        pack_first[q] = first
        pack_last[q] = last

    band = band_matrix()

    def side_copy(index, dx, dy):
        source, target = (pack_first, after) if dy < 0 else (pack_last, before)
        at, length, to = {0: (0, own, w), -1: (w, w, w + own), 1: (own, w, 0)}[dx]
        if dx != 0:
            source = target
        return pltpu.make_async_remote_copy(
            src_ref=source.at[:, pl.ds(at, length), :],
            dst_ref=target.at[:, pl.ds(to, length), :],
            send_sem=send_s.at[index], recv_sem=recv_s.at[index],
            device_id=device(dx, 0 if dx else dy), device_id_type=MESH,
        )

    def row_copy(index, dx, chunk):
        at, to = (0, w + own) if dx < 0 else (own - w, 0)
        return pltpu.make_async_remote_copy(
            src_ref=main.at[pl.ds(chunk * CHUNK + DIP_HALF, CHUNK), pl.ds(w + at, w), :],
            dst_ref=main.at[pl.ds(chunk * CHUNK + DIP_HALF, CHUNK), pl.ds(to, w), :],
            send_sem=send_x.at[index, chunk], recv_sem=recv_x.at[index, chunk],
            device_id=device(dx, 0), device_id_type=MESH,
        )

    sides = [(0, -1), (0, 1), (-1, -1), (-1, 1), (1, -1), (1, 1)]
    expected = sum(jnp.where(there, 1, 0) for there in faces.values())
    pl.semaphore_wait(barrier, expected)
    def send_sides(corners):
        for index, (dx, dy) in enumerate(sides):
            if (dx != 0) == corners:
                @pl.when(exists[dx, -dy] if corners else exists[dx, dy])
                def _(index=index, dx=dx, dy=dy):
                    side_copy(index, dx, dy).start()

    def send_rows(first, last):
        for chunk in range(first, last):
            for index, dx in enumerate((-1, 1)):
                @pl.when(exists[dx, 0])
                def _(index=index, dx=dx, chunk=chunk):
                    row_copy(index, dx, chunk).start()

    send_rows(0, chunks // 2)
    send_sides(False)

    def arrive(corners):
        for index, (dx, dy) in enumerate(sides):
            if (dx != 0) == corners:
                @pl.when(exists[-dx, -dy])
                def _(index=index, dx=dx, dy=dy):
                    side_copy(index, dx, dy).wait_recv()

    def unpack(at, length):
        lane = lax.broadcasted_iota(jnp.int32, (length, LANES), 1)
        for q in range(depth // GROUP):
            right = after[q, pl.ds(at, length), :]
            left = before[q, pl.ds(at, length), :]
            for j in range(GROUP):
                a = pltpu.roll(right, (LANES - SIDE * j) % LANES, 1)
                b = pltpu.roll(left, (2 * LANES - SIDE - SIDE * j) % LANES, 1)
                halo[q * GROUP + j + DIP_HALF, pl.ds(at, length), :] = jnp.where(
                    lane < SIDE, a, jnp.where(lane >= LANES - SIDE, b, 0.0)
                )

    arrive(False)
    send_sides(True)
    send_rows(chunks // 2, chunks - 1)
    unpack(w, own)
    send_rows(chunks - 1, chunks)

    shear = ((sl_m, sl_h), (sr_m, sr_h))
    shear_row = ((rl_m, rl_h), (rr_m, rr_h))

    squares = (square_0, square_1, square_2)

    @pl.loop(0, chunks + 1)
    def _(chunk):
        @pl.when(chunk < chunks)
        def _():
            prepare_own(chunk, rows, main, halo, box, shear, band)

        @pl.when(chunk > 0)
        def _():
            finish_own(chunk - 1, rows, main, halo, box, shear, squares, band, out_ref)

    arrive(True)
    unpack(0, w)
    unpack(w + own, w)

    @pl.loop(0, chunks + 1)
    def _(chunk):
        @pl.when(chunk < chunks)
        def _():
            for index, dx in enumerate((-1, 1)):
                @pl.when(exists[-dx, 0])
                def _(index=index, dx=dx):
                    row_copy(index, dx, chunk).wait_recv()
            prepare(chunk, rows, main, halo, box, row, shear, shear_row, band)

        @pl.when(chunk > 0)
        def _():
            finish(chunk - 1, rows, main, halo, box, row, shear, shear_row, squares, band, out_ref)

    for index, (dx, dy) in enumerate(sides):
        @pl.when(exists[dx, -dy] if dx else exists[dx, dy])
        def _(index=index, dx=dx, dy=dy):
            side_copy(index, dx, dy).wait_send()
    for chunk in range(chunks):
        for index, dx in enumerate((-1, 1)):
            @pl.when(exists[dx, 0])
            def _(index=index, dx=dx, chunk=chunk):
                row_copy(index, dx, chunk).wait_send()


def shards(image):
    depth, own, width = image.shape
    rows = own + 2 * STRIKE_HALF
    planes = depth + 2 * DIP_HALF
    full = pltpu.VMEM((planes, rows, LANES), F32)
    part = pltpu.VMEM((planes, own, LANES), F32)
    groups = depth // GROUP
    semblance = pl.pallas_call(
        functools.partial(kernel, lax.axis_size("gx"), lax.axis_size("gy")),
        out_shape=jax.ShapeDtypeStruct(image.shape, F32),
        in_specs=[pl.BlockSpec(memory_space=pltpu.HBM)],
        out_specs=pl.BlockSpec(memory_space=pltpu.VMEM),
        scratch_shapes=[full, full, full, part] + [full] * 4 + [part] * 4
        + [pltpu.VMEM(image.shape, F32)] * 3
        + [pltpu.VMEM((groups, own, LANES), F32)] * 2
        + [pltpu.VMEM((groups, rows, LANES), F32)] * 2
        + [pltpu.SemaphoreType.DMA((2, depth // CHUNK))] * 2
        + [pltpu.SemaphoreType.DMA((6,))] * 2 + [pltpu.SemaphoreType.DMA],
        compiler_params=pltpu.CompilerParams(
            vmem_limit_bytes=40 * 1024 * 1024, collective_id=0, has_side_effects=True
        ),
    )(image)
    return 1.0 - semblance


def solution(mesh):
    spec = P(None, "gx", "gy")
    return jax.shard_map(shards, mesh=mesh, in_specs=(spec,), out_specs=spec, check_vma=False)
```

profile of v0, /device:TPU:25, one launch (start us, length us, event | category | flops | bytes accessed | tf_op | source)
XLA Modules:
  0.0 14.3 jit_solution(17667906841662511344)
XLA Ops:
  0.0 0.0 copy-start
  0.0 0.9 %copy-done = f32[32,16,128]{2,1,0:T(8,128)S(1)} copy-done((f32[32,16,128]{2,1,0:T(8,128)S(1)}, f32[32,16,128]{2,1,0:T(8,128)}, u32[]{:S(2)}) %copy-start) | copy-done | bytes 262168
  1.0 12.6 %shard_map.17 = f32[32,16,128]{2,1,0:T(8,128)S(1)} custom-call(f32[32,16,128]{2,1,0:T(8,128)S(1)} %copy-done), custom_call_target="tpu_custom_call" | custom-call | tf_op jit(solution)/shard_map/pallas_call | solution.py:415
  13.5 0.7 %broadcast_subtract_fusion = f32[32,16,128]{2,1,0:T(8,128)} fusion(f32[32,16,128]{2,1,0:T(8,128)S(1)} %shard_map.17), kind=kLoop, calls=%fused_computation | loop fusion | flops 65536 | bytes 524288 | tf_op jit(solution)/shard_map/sub | solution.py:430
Async XLA Ops:
  0.0 0.9 %copy-start = (f32[32,16,128]{2,1,0:T(8,128)S(1)}, f32[32,16,128]{2,1,0:T(8,128)}, u32[]{:S(2)}) copy-start(f32[32,16,128]{2,1,0:T(8,128)} %image_ref.1) | copy-start | bytes 786436
where the time goes:
time: 14.4 us; the launch traced here: 14.3 us
  Pallas kernels  12.6 us (88%)
  local copies, waits for them, and re-layouts  0.95 us (7%)
  other arithmetic  0.72 us (5%)
    pallas_call x1, Pallas kernels, shards(): pl.pallas_call(functools.partial(kernel, lax.axis_size('gx'), lax.axis_si...  12.6 us
    unnamed x2, local copies, waits for them, and re-layouts  0.95 us
    sub x1, other arithmetic, shards(): return 1.0 - semblance  0.72 us

commit v1 on v0

--- a/solution.py
+++ b/solution.py
@@ -426,7 +426,7 @@
         compiler_params=pltpu.CompilerParams(
             vmem_limit_bytes=40 * 1024 * 1024, collective_id=0, has_side_effects=True
         ),
-    )(image)
+    )(pltpu.with_memory_space_constraint(image, pltpu.HBM))
     return 1.0 - semblance
 
 

time: 14.4 us -> 13.3 us (0.924)
  local copies, waits for them, and re-layouts: 0.95 us -> 0 us
  Pallas kernels: 12.6 us -> 12.4 us
    unnamed x2 -> x0, local copies, waits for them, and re-layouts: 0.95 us -> none
where the time goes in v1:
time: 13.3 us; the launch traced here: 13.2 us
  Pallas kernels  12.4 us (93%)
  other arithmetic  0.72 us (5%)
    pallas_call x1, Pallas kernels, shards(): pl.pallas_call(functools.partial(kernel, lax.axis_size('gx'), lax.axis_si...  12.4 us
    sub x1, other arithmetic, shards(): return 1.0 - semblance  0.72 us

profile of v1, /device:TPU:25, one launch (start us, length us, event | category | flops | bytes accessed | tf_op | source)
XLA Modules:
  0.0 13.2 jit_solution(8124725192169224132)
XLA Ops:
  0.0 12.4 %shard_map.17 = f32[32,16,128]{2,1,0:T(8,128)S(1)} custom-call(f32[32,16,128]{2,1,0:T(8,128)} %image_ref.1), custom_call_target="tpu_custom_call" | custom-call | tf_op jit(solution)/shard_map/pallas_call | solution.py:415
  12.5 0.7 %broadcast_subtract_fusion = f32[32,16,128]{2,1,0:T(8,128)} fusion(f32[32,16,128]{2,1,0:T(8,128)S(1)} %shard_map.17), kind=kLoop, calls=%fused_computation | loop fusion | flops 65536 | bytes 524288 | tf_op jit(solution)/shard_map/sub | solution.py:430
